TPU v7x, 32 devices: a whole 2x2x4 slice. The times are simulated.
32 devices in a mesh: grp: 8 (over y, x, core), sub: 4 (over z).
Axes of the slice: x: 2, y: 2, z: 4, core: 2. Of those that a mesh axis runs over, the one named last changes fastest.
Arguments:
- master: float32 [4096, 3584], P(('grp', 'sub')), may hold values from -120 to 120
- moment_one: float32 [4096, 3584], P(('grp', 'sub')), may hold values from -6 to 6
- moment_two: float32 [4096, 3584], P(('grp', 'sub')), may hold values from 0.01 to 4
- gradient: float32 [4096, 3584], P(('grp', 'sub')), may hold values from -120 to 120
- partner: int32 [32], replicated, may hold values from 0 to 31, each once
- tensor_of_row: int32 [4096], replicated, may hold values from 0 to 7, never falling along the last dimension, each value on 1 to 1024 neighbouring positions
Outputs:
- new_master: float32 [4096, 3584], P(('grp', 'sub'))
- new_moment_one: float32 [4096, 3584], P(('grp', 'sub'))
- new_moment_two: float32 [4096, 3584], P(('grp', 'sub'))
Inputs may be any that keep to these rules, and one draw needn't show every extreme that they name: partner[n] is the device of new rank n; every device holds exactly one rank. `tensor_of_row`: tensor numbers never fall along the rows; each of the 8 tensors has one or more rows.
All inputs are finite; a program needn't handle non-finite values.
Results may differ from a plain program's by a relative error of at most 0.00007.
Values sent between devices are 32-bit elements; how exact they have to be, the bound alone decides.
A program may use at most 128 MiB of HBM per device.

v0:
```python
import jax
import jax.numpy as jnp
from jax import lax
from jax.sharding import PartitionSpec as P

LAYERS = 8
beta_one = 0.9
beta_two = 0.999
step_count = 10
adam_eps = 1e-06
trust_eps = 1e-06
learn_rate = 0.05
decay_rate = 0.01


def tensor_totals(values, onehot):
    return jnp.dot(values[None, :], onehot, precision=lax.Precision.HIGHEST)[0]


def local(master, moment_one, moment_two, gradient, partner, tensor_of_row):
    rows_dev, width = master.shape
    devices = lax.axis_size(("grp", "sub"))
    block = rows_dev // devices
    device_id = lax.axis_index(("grp", "sub"))
    numbers = jnp.arange(devices, dtype=jnp.int32)
    matches = partner[None, :] == numbers[:, None]
    inverse = jnp.sum(jnp.where(matches, numbers[None, :], 0), axis=1)
    my_rank = lax.dynamic_index_in_dim(inverse, device_id, 0, keepdims=False)
    layer_ids = jnp.arange(LAYERS, dtype=jnp.int32)
    id_grid = tensor_of_row.reshape(devices, devices, block)
    new_ids = lax.dynamic_index_in_dim(id_grid, my_rank, 1, keepdims=False).reshape(rows_dev)
    new_hot = (new_ids[:, None] == layer_ids[None, :]).astype(jnp.float32)
    old_ids = lax.dynamic_slice_in_dim(tensor_of_row, device_id * rows_dev, rows_dev)
    old_hot = (old_ids[:, None] == layer_ids[None, :]).astype(jnp.float32)
    weight_sq = lax.psum(tensor_totals(jnp.sum(master * master, axis=1), old_hot), ("grp", "sub"))

    def outbound(values):
        return jnp.take(values.reshape(devices, block, width), inverse, axis=0)

    sending = (outbound(master), outbound(moment_one), outbound(moment_two))
    arrived = (
        lax.all_to_all(sending[0], ("grp", "sub"), split_axis=0, concat_axis=0, tiled=True),
        lax.all_to_all(sending[1], ("grp", "sub"), split_axis=0, concat_axis=0, tiled=True),
        lax.all_to_all(sending[2], ("grp", "sub"), split_axis=0, concat_axis=0, tiled=True),
    )
    weights, moment_old, square_old = [piece.reshape(rows_dev, width) for piece in arrived]
    first = beta_one * moment_old + (1.0 - beta_one) * gradient
    second = beta_two * square_old + (1.0 - beta_two) * gradient * gradient
    correct_one = 1.0 - beta_one**step_count
    correct_two = 1.0 - beta_two**step_count
    update = (
        first / correct_one / (jnp.sqrt(second / correct_two) + adam_eps) + decay_rate * weights
    )
    update_local = tensor_totals(jnp.sum(update * update, axis=1), new_hot)
    update_sq = lax.psum(update_local, ("grp", "sub"))
    ratio = jnp.sqrt(weight_sq) / (jnp.sqrt(update_sq) + trust_eps)
    row_ratio = jnp.dot(new_hot, ratio[:, None], precision=lax.Precision.HIGHEST)
    fresh = weights - learn_rate * row_ratio * update
    return (fresh, first, second)


def solution(mesh):
    return jax.shard_map(
        local,
        mesh=mesh,
        in_specs=(
            P(("grp", "sub"), None),
            P(("grp", "sub"), None),
            P(("grp", "sub"), None),
            P(("grp", "sub"), None),
            P(),
            P(),
        ),
        out_specs=(P(("grp", "sub"), None), P(("grp", "sub"), None), P(("grp", "sub"), None)),
        check_vma=False,
    )
```

profile of v0, /device:TPU:0, one launch (start us, length us, event | category | flops | bytes accessed | tf_op | source)
XLA Modules:
  0.0 219.0 jit_solution(205470790843580463)
XLA Ops:
  0.6 0.8 select_reduce_fusion
  1.4 1.9 reshape.52
  3.3 2.8 %reshape.53 = f32[32,4,3584]{2,1,0:T(4,128)} reshape(f32[128,3584]{1,0:T(8,128)} %param.10) | data formatting | bytes 3670016 | tf_op jit(solution)/shard_map/reshape | solution.py:38
  6.2 2.8 %gather_fusion.1 = f32[32,4,3584]{2,1,0:T(4,128)} fusion(f32[32,4,3584]{2,1,0:T(4,128)S(1)} %reshape.52, s32[1024]{0:T(1024)S(1)} %pad_clamp_fusion), kind=kCustom, calls=%fused_computation.1.clone | custom fusion | bytes 3670144 | tf_op jit(solution)/shard_map/jit(_take)/gather | solution.py:38
  8.9 4.4 %gather_fusion.2 = f32[32,4,3584]{2,1,0:T(4,128)} fusion(f32[32,4,3584]{2,1,0:T(4,128)} %reshape.53, s32[1024]{0:T(1024)S(1)} %pad_clamp_fusion), kind=kCustom, calls=%fused_computation.2.clone | custom fusion | bytes 3670144 | tf_op jit(solution)/shard_map/jit(_take)/gather | solution.py:38
  13.3 0.0 copy-done.1
  13.3 1.8 reshape.49
  15.1 4.4 %gather_fusion = f32[32,4,3584]{2,1,0:T(4,128)} fusion(f32[32,4,3584]{2,1,0:T(4,128)} %reshape.49, s32[1024]{0:T(1024)S(1)} %pad_clamp_fusion), kind=kCustom, calls=%fused_computation.clone | custom fusion | bytes 3670144 | tf_op jit(solution)/shard_map/jit(_take)/gather | solution.py:38
  19.5 0.0 copy-done.2
  19.5 4.6 %broadcast_select_fusion = (f32[32,4,3584]{2,1,0:T(4,128)S(1)}, f32[32,4,3584]{2,1,0:T(4,128)S(1)}, f32[32,4,3584]{2,1,0:T(4,128)}) fusion(f32[32,4,3584]{2,1,0:T(4,128)} %gather_fusion.2, pred[32]{0:T(512)(128)(4,1)S(1)} %compare_and_fusion, f32[32,4,3584]{2,1,0:T(4,128)S(1)} %copy-done.2, f32[32,4,3584]{2,1,0:T(4,128)} %gather_fusion), kind=kLoop, calls=%fused_computation.14 | loop fusion | flops 1376256 | bytes 11010080 | tf_op jit(solution)/shard_map/jit(_take)/select_n | solution.py:38
  24.1 49.2 %all_to_all.15 = f32[32,4,3584]{2,1,0:T(4,128)} all-to-all(f32[32,4,3584]{2,1,0:T(4,128)S(1)} %get-tuple-element.9), channel_id=1, replica_groups=mesh['grp'=8,'sub'=4] {'grp','sub'}, dimensions={0} | all-to-all | bytes 3670016 | tf_op jit(solution)/shard_map/all_to_all | solution.py:44
  73.3 46.2 %all_to_all.16 = f32[32,4,3584]{2,1,0:T(4,128)S(1)} all-to-all(f32[32,4,3584]{2,1,0:T(4,128)S(1)} %get-tuple-element.10), channel_id=1, replica_groups=mesh['grp'=8,'sub'=4] {'grp','sub'}, dimensions={0} | all-to-all | bytes 3670016 | tf_op jit(solution)/shard_map/all_to_all | solution.py:43
  119.5 4.8 %all-to-all-start = ((f32[32,4,3584]{2,1,0:T(4,128)}), f32[32,4,3584]{2,1,0:T(4,128)}, u32[]{:S(2)}, u32[]{:S(2)}) async-start(f32[32,4,3584]{2,1,0:T(4,128)} %get-tuple-element.11), calls=%async_computation | async-start | bytes 3670016 | tf_op jit(solution)/shard_map/all_to_all | solution.py:42
  124.3 0.6 dynamic_slice.11
  126.2 0.5 reshape.51
  126.7 0.1 dynamic_slice.13
  127.5 0.1 dynamic-slice_reduce_fusion
  127.5 0.1 eq.44
  127.7 1.8 multiply_reduce_fusion.1
  129.5 0.2 convolution_bitcast_fusion.2
  129.7 0.0 copy-done
  129.7 1.7 broadcast_multiply_fusion
  131.4 2.9 %mul.76 = f32[128,3584]{1,0:T(8,128)} reshape(f32[32,4,3584]{2,1,0:T(4,128)} %broadcast_multiply_fusion) | data formatting | bytes 3670016 | tf_op jit(solution)/shard_map/mul | solution.py:48
  134.3 1.7 broadcast_multiply_fusion.1
  136.0 2.9 %mul.71 = f32[128,3584]{1,0:T(8,128)} reshape(f32[32,4,3584]{2,1,0:T(4,128)} %broadcast_multiply_fusion.1) | data formatting | bytes 3670016 | tf_op jit(solution)/shard_map/mul | solution.py:47
  138.9 26.5 %all-to-all-done = f32[32,4,3584]{2,1,0:T(4,128)} async-done(((f32[32,4,3584]{2,1,0:T(4,128)}), f32[32,4,3584]{2,1,0:T(4,128)}, u32[]{:S(2)}, u32[]{:S(2)}) %all-to-all-start) | async-done | bytes 1835040 | tf_op jit(solution)/shard_map/all_to_all | solution.py:42
  165.4 1.9 reshape.50
  167.3 5.7 %multiply_reduce_fusion = (f32[128]{0:T(128)S(1)}, f32[128,3584]{1,0:T(8,128)}, f32[128,3584]{1,0:T(8,128)}) fusion(f32[128,3584]{1,0:T(8,128)S(1)} %reshape.50, f32[128,3584]{1,0:T(8,128)} %mul.71, f32[128,3584]{1,0:T(8,128)} %param.11, f32[128,3584]{1,0:T(8,128)} %mul.76), kind=kLoop, calls=%fused_computation.6 | loop fusion | flops 5963648 | bytes 11010560 | tf_op jit(solution)/shard_map/reduce_sum | solution.py:54
  173.0 0.2 convolution_bitcast_fusion.1
  173.2 41.3 %all-reduce = (f32[8]{0:T(128)S(1)}, f32[8]{0:T(128)S(1)}) all-reduce(f32[8]{0:T(128)S(1)} %convolution_bitcast_fusion.1, f32[8]{0:T(128)S(1)} %convolution_bitcast_fusion.2), channel_id=1, replica_groups=mesh['grp'=8,'sub'=4] {'grp','sub'}, use_global_device_ids=true, to_apply=%region_4.6 | all-reduce | flops 16 | bytes 128 | tf_op jit(solution)/shard_map/psum | solution.py:55
  214.5 0.2 fusion.1
  214.7 4.3 %multiply_subtract_fusion = f32[128,3584]{1,0:T(8,128)} fusion(f32[128,3584]{1,0:T(8,128)S(1)} %reshape.50, f32[128]{0:T(128)S(1)} %fusion.1, f32[128,3584]{1,0:T(8,128)} %get-tuple-element.8, f32[128,3584]{1,0:T(8,128)} %get-tuple-element.7), kind=kLoop, calls=%fused_computation.5 | loop fusion | flops 3670016 | bytes 7340544 | tf_op jit(solution)/shard_map/sub | solution.py:58
  (8 shorter events, 0.0 us)
Async XLA Ops:
  8.9 4.4 %copy-start.1 = (f32[128,3584]{1,0:T(8,128)S(1)}, f32[128,3584]{1,0:T(8,128)}, u32[]{:S(2)}) copy-start(f32[128,3584]{1,0:T(8,128)} %param.8) | copy-start | bytes 5505028
  15.1 4.4 %copy-start.2 = (f32[32,4,3584]{2,1,0:T(4,128)S(1)}, f32[32,4,3584]{2,1,0:T(4,128)}, u32[]{:S(2)}) copy-start(f32[32,4,3584]{2,1,0:T(4,128)} %gather_fusion.1) | copy-start | bytes 5505028
  119.5 6.7 %copy-start.3 = (s32[4096]{0:T(1024)S(1)}, s32[4096]{0:T(1024)}, u32[]{:S(2)}) copy-start(s32[4096]{0:T(1024)} %param.13) | copy-start | bytes 49156
  119.5 45.8 %all-to-all-start = ((f32[32,4,3584]{2,1,0:T(4,128)}), f32[32,4,3584]{2,1,0:T(4,128)}, u32[]{:S(2)}, u32[]{:S(2)}) async-start(f32[32,4,3584]{2,1,0:T(4,128)} %get-tuple-element.11), calls=%async_computation | async-start | bytes 3670016 | tf_op jit(solution)/shard_map/all_to_all | solution.py:42
  127.6 2.1 copy-start
where the time goes:
time: 219 us
  blocking collectives  137 us (63%)
  local copies, waits for them, and re-layouts  27.1 us (12%)
  waiting for transfers between devices  26.5 us (12%)
  other arithmetic  20.7 us (9%)
  starting transfers between devices  4.76 us (2%)
  between operations  2.68 us (1%)
    all_to_all x1, blocking collectives, local(): lax.all_to_all(sending[2], ('grp', 'sub'), split_axis=0, concat_axis=0, t...  49.2 us
    all_to_all x1, blocking collectives, local(): lax.all_to_all(sending[1], ('grp', 'sub'), split_axis=0, concat_axis=0, t...  46.2 us
    psum x1, blocking collectives, local(): update_sq = lax.psum(update_local, ('grp', 'sub'))  41.3 us
    all_to_all x1, waiting for transfers between devices, local(): lax.all_to_all(sending[0], ('grp', 'sub'), split_axis=0, concat_axis=0, t...  26.5 us
    gather x3, local copies, waits for them, and re-layouts, outbound(): return jnp.take(values.reshape(devices, block, width), inverse, axis=0)  11.6 us
    reshape x3, local copies, waits for them, and re-layouts, outbound(): return jnp.take(values.reshape(devices, block, width), inverse, axis=0)  6.49 us
    reduce_sum x1, other arithmetic, local(): update_local = tensor_totals(jnp.sum(update * update, axis=1), new_hot)  5.68 us
    all_to_all x1, starting transfers between devices, local(): lax.all_to_all(sending[0], ('grp', 'sub'), split_axis=0, concat_axis=0, t...  4.76 us
  transfers between devices with their start and end apart: 1, of which 1 were waited for; matrix products, arithmetic and copies ran while one was open for 6% of the time, Pallas kernels for 0%

commit v1 on v0

--- a/solution.py
+++ b/solution.py
@@ -52,7 +52,7 @@
         first / correct_one / (jnp.sqrt(second / correct_two) + adam_eps) + decay_rate * weights
     )
     update_local = tensor_totals(jnp.sum(update * update, axis=1), new_hot)
-    update_sq = lax.psum(update_local, ("grp", "sub"))
+    update_sq = lax.psum(lax.psum(update_local, axis_name="sub"), "grp")
     ratio = jnp.sqrt(weight_sq) / (jnp.sqrt(update_sq) + trust_eps)
     row_ratio = jnp.dot(new_hot, ratio[:, None], precision=lax.Precision.HIGHEST)
     fresh = weights - learn_rate * row_ratio * update

time: 219 us -> 240 us (1.096)
  blocking collectives: 137 us -> 157 us
    psum x1 -> x3, blocking collectives: 41.3 us -> 61.7 us  [the longest x1 37 us: local(): lax.psum(tensor_totals(jnp.sum(master * master, axis=1), old_hot), ('grp'...]
  transfers between devices with their start and end apart: 1 -> 1, of which waited for: 1 -> 1; matrix products, arithmetic and copies ran while one was open for 6% -> 5% of each run, Pallas kernels for 0% -> 0%
where the time goes in v1:
time: 240 us
  blocking collectives  157 us (65%)
  local copies, waits for them, and re-layouts  27.3 us (11%)
  waiting for transfers between devices  26.5 us (11%)
  other arithmetic  20.7 us (9%)
  starting transfers between devices  4.76 us (2%)
  between operations  2.68 us (1%)
    all_to_all x1, blocking collectives, local(): lax.all_to_all(sending[2], ('grp', 'sub'), split_axis=0, concat_axis=0, t...  49.2 us
    all_to_all x1, blocking collectives, local(): lax.all_to_all(sending[1], ('grp', 'sub'), split_axis=0, concat_axis=0, t...  46.2 us
    psum x1, blocking collectives, local(): lax.psum(tensor_totals(jnp.sum(master * master, axis=1), old_hot), ('grp'...  37 us
    all_to_all x1, waiting for transfers between devices, local(): lax.all_to_all(sending[0], ('grp', 'sub'), split_axis=0, concat_axis=0, t...  26.5 us
    psum x2, blocking collectives, local(): update_sq = lax.psum(lax.psum(update_local, axis_name='sub'), 'grp')  24.7 us
    gather x3, local copies, waits for them, and re-layouts, outbound(): return jnp.take(values.reshape(devices, block, width), inverse, axis=0)  11.6 us
    reshape x3, local copies, waits for them, and re-layouts, outbound(): return jnp.take(values.reshape(devices, block, width), inverse, axis=0)  6.49 us
    reduce_sum x1, other arithmetic, local(): update_local = tensor_totals(jnp.sum(update * update, axis=1), new_hot)  5.68 us
  transfers between devices with their start and end apart: 1, of which 1 were waited for; matrix products, arithmetic and copies ran while one was open for 5% of the time, Pallas kernels for 0%

profile of v1, /device:TPU:0, one launch (start us, length us, event | category | flops | bytes accessed | tf_op | source)
XLA Modules:
  0.0 239.6 jit_solution(2474067026728267458)
XLA Ops:
  0.6 0.8 select_reduce_fusion
  1.4 1.9 reshape.52
  3.3 2.8 %reshape.53 = f32[32,4,3584]{2,1,0:T(4,128)} reshape(f32[128,3584]{1,0:T(8,128)} %param.10) | data formatting | bytes 3670016 | tf_op jit(solution)/shard_map/reshape | solution.py:38
  6.2 2.8 %gather_fusion.1 = f32[32,4,3584]{2,1,0:T(4,128)} fusion(f32[32,4,3584]{2,1,0:T(4,128)S(1)} %reshape.52, s32[1024]{0:T(1024)S(1)} %pad_clamp_fusion), kind=kCustom, calls=%fused_computation.1.clone | custom fusion | bytes 3670144 | tf_op jit(solution)/shard_map/jit(_take)/gather | solution.py:38
  8.9 4.4 %gather_fusion.2 = f32[32,4,3584]{2,1,0:T(4,128)} fusion(f32[32,4,3584]{2,1,0:T(4,128)} %reshape.53, s32[1024]{0:T(1024)S(1)} %pad_clamp_fusion), kind=kCustom, calls=%fused_computation.2.clone | custom fusion | bytes 3670144 | tf_op jit(solution)/shard_map/jit(_take)/gather | solution.py:38
  13.3 1.8 reshape.49
  15.1 4.4 %gather_fusion = f32[32,4,3584]{2,1,0:T(4,128)} fusion(f32[32,4,3584]{2,1,0:T(4,128)} %reshape.49, s32[1024]{0:T(1024)S(1)} %pad_clamp_fusion), kind=kCustom, calls=%fused_computation.clone | custom fusion | bytes 3670144 | tf_op jit(solution)/shard_map/jit(_take)/gather | solution.py:38
  19.5 4.6 %broadcast_select_fusion = (f32[32,4,3584]{2,1,0:T(4,128)S(1)}, f32[32,4,3584]{2,1,0:T(4,128)S(1)}, f32[32,4,3584]{2,1,0:T(4,128)}) fusion(f32[32,4,3584]{2,1,0:T(4,128)} %gather_fusion.2, pred[32]{0:T(512)(128)(4,1)S(1)} %compare_and_fusion, f32[32,4,3584]{2,1,0:T(4,128)S(1)} %copy-done.2, f32[32,4,3584]{2,1,0:T(4,128)} %gather_fusion), kind=kLoop, calls=%fused_computation.14 | loop fusion | flops 1376256 | bytes 11010080 | tf_op jit(solution)/shard_map/jit(_take)/select_n | solution.py:38
  24.1 49.2 %all_to_all.15 = f32[32,4,3584]{2,1,0:T(4,128)} all-to-all(f32[32,4,3584]{2,1,0:T(4,128)S(1)} %get-tuple-element.7), channel_id=1, replica_groups=mesh['grp'=8,'sub'=4] {'grp','sub'}, dimensions={0} | all-to-all | bytes 3670016 | tf_op jit(solution)/shard_map/all_to_all | solution.py:44
  73.3 46.2 %all_to_all.16 = f32[32,4,3584]{2,1,0:T(4,128)S(1)} all-to-all(f32[32,4,3584]{2,1,0:T(4,128)S(1)} %get-tuple-element.8), channel_id=1, replica_groups=mesh['grp'=8,'sub'=4] {'grp','sub'}, dimensions={0} | all-to-all | bytes 3670016 | tf_op jit(solution)/shard_map/all_to_all | solution.py:43
  119.5 4.8 %all-to-all-start = ((f32[32,4,3584]{2,1,0:T(4,128)}), f32[32,4,3584]{2,1,0:T(4,128)}, u32[]{:S(2)}, u32[]{:S(2)}) async-start(f32[32,4,3584]{2,1,0:T(4,128)} %get-tuple-element.9), calls=%async_computation | async-start | bytes 3670016 | tf_op jit(solution)/shard_map/all_to_all | solution.py:42
  124.3 0.6 dynamic_slice.11
  126.2 0.5 reshape.51
  126.7 0.1 dynamic_slice.13
  127.5 0.1 dynamic-slice_reduce_fusion
  127.5 0.1 eq.44
  127.7 1.8 multiply_reduce_fusion.1
  129.5 0.2 copy-done
  129.7 1.7 broadcast_multiply_fusion
  131.4 2.9 %mul.76 = f32[128,3584]{1,0:T(8,128)} reshape(f32[32,4,3584]{2,1,0:T(4,128)} %broadcast_multiply_fusion) | data formatting | bytes 3670016 | tf_op jit(solution)/shard_map/mul | solution.py:48
  134.3 1.7 broadcast_multiply_fusion.1
  136.0 2.9 %mul.71 = f32[128,3584]{1,0:T(8,128)} reshape(f32[32,4,3584]{2,1,0:T(4,128)} %broadcast_multiply_fusion.1) | data formatting | bytes 3670016 | tf_op jit(solution)/shard_map/mul | solution.py:47
  138.9 26.5 %all-to-all-done = f32[32,4,3584]{2,1,0:T(4,128)} async-done(((f32[32,4,3584]{2,1,0:T(4,128)}), f32[32,4,3584]{2,1,0:T(4,128)}, u32[]{:S(2)}, u32[]{:S(2)}) %all-to-all-start) | async-done | bytes 1835040 | tf_op jit(solution)/shard_map/all_to_all | solution.py:42
  165.4 1.9 reshape.50
  167.3 5.7 %multiply_reduce_fusion = (f32[128]{0:T(128)S(1)}, f32[128,3584]{1,0:T(8,128)}, f32[128,3584]{1,0:T(8,128)}) fusion(f32[128,3584]{1,0:T(8,128)S(1)} %reshape.50, f32[128,3584]{1,0:T(8,128)} %mul.71, f32[128,3584]{1,0:T(8,128)} %param.11, f32[128,3584]{1,0:T(8,128)} %mul.76), kind=kLoop, calls=%fused_computation.6 | loop fusion | flops 5963648 | bytes 11010560 | tf_op jit(solution)/shard_map/reduce_sum | solution.py:54
  173.0 0.2 convolution_bitcast_fusion.1
  173.2 0.2 convolution_bitcast_fusion.2
  173.4 12.0 %psum.22 = f32[8]{0:T(128)S(1)} all-reduce(f32[8]{0:T(128)S(1)} %convolution_bitcast_fusion.1), channel_id=1, replica_groups=mesh['grp'=8,'sub'=4] {'sub'}, use_global_device_ids=true, to_apply=%region_4.6 | all-reduce | flops 8 | bytes 64 | tf_op jit(solution)/shard_map/psum | solution.py:55
  185.4 37.0 %psum.21 = f32[8]{0:T(128)S(1)} all-reduce(f32[8]{0:T(128)S(1)} %convolution_bitcast_fusion.2), channel_id=1, replica_groups=mesh['grp'=8,'sub'=4] {'grp','sub'}, use_global_device_ids=true, to_apply=%region_2.4 | all-reduce | flops 8 | bytes 64 | tf_op jit(solution)/shard_map/psum | solution.py:35
  222.4 12.7 %psum.23 = f32[8]{0:T(128)S(1)} all-reduce(f32[8]{0:T(128)S(1)} %psum.22), channel_id=1, replica_groups=mesh['grp'=8,'sub'=4] {'grp'}, use_global_device_ids=true, to_apply=%region_5.7 | all-reduce | flops 8 | bytes 64 | tf_op jit(solution)/shard_map/psum | solution.py:55
  235.1 0.2 fusion.1
  235.3 4.3 %multiply_subtract_fusion = f32[128,3584]{1,0:T(8,128)} fusion(f32[128,3584]{1,0:T(8,128)S(1)} %reshape.50, f32[128]{0:T(128)S(1)} %fusion.1, f32[128,3584]{1,0:T(8,128)} %get-tuple-element.6, f32[128,3584]{1,0:T(8,128)} %get-tuple-element.5), kind=kLoop, calls=%fused_computation.5 | loop fusion | flops 3670016 | bytes 7340544 | tf_op jit(solution)/shard_map/sub | solution.py:58
  (10 shorter events, 0.0 us)
Async XLA Ops:
  8.9 4.4 %copy-start.1 = (f32[128,3584]{1,0:T(8,128)S(1)}, f32[128,3584]{1,0:T(8,128)}, u32[]{:S(2)}) copy-start(f32[128,3584]{1,0:T(8,128)} %param.8) | copy-start | bytes 5505028
  15.1 4.4 %copy-start.2 = (f32[32,4,3584]{2,1,0:T(4,128)S(1)}, f32[32,4,3584]{2,1,0:T(4,128)}, u32[]{:S(2)}) copy-start(f32[32,4,3584]{2,1,0:T(4,128)} %gather_fusion.1) | copy-start | bytes 5505028
  119.5 6.7 %copy-start.3 = (s32[4096]{0:T(1024)S(1)}, s32[4096]{0:T(1024)}, u32[]{:S(2)}) copy-start(s32[4096]{0:T(1024)} %param.13) | copy-start | bytes 49156
  119.5 45.8 %all-to-all-start = ((f32[32,4,3584]{2,1,0:T(4,128)}), f32[32,4,3584]{2,1,0:T(4,128)}, u32[]{:S(2)}, u32[]{:S(2)}) async-start(f32[32,4,3584]{2,1,0:T(4,128)} %get-tuple-element.9), calls=%async_computation | async-start | bytes 3670016 | tf_op jit(solution)/shard_map/all_to_all | solution.py:42
  127.6 2.1 copy-start
